TPU v7x, 128 devices: a whole 4x4x4 slice. The times are simulated.
128 devices in a mesh: row: 8 (over z, core), col: 16 (over x, y).
Axes of the slice: x: 4, y: 4, z: 4, core: 2. Of those that a mesh axis runs over, the one named last changes fastest.
Arguments:
- right_side: float32 [16, 2048, 6144], P(None, 'row', 'col'), may hold values from -100 to 100
- cond_x: float32 [2048, 6144], P('row', 'col'), may hold values from 0.25 to 4
- cond_y: float32 [2048, 6144], P('row', 'col'), may hold values from 0.25 to 4
- pad_mask: int32 [2048, 6144], P('row', 'col'), may hold values 0 or 1
Outputs:
- solution: float32 [16, 2048, 6144], P(None, 'row', 'col')
- residual: float32 [16, 2048, 6144], P(None, 'row', 'col')
All inputs are finite; a program needn't handle non-finite values. No bound on the sum of `pad_mask` on one device may be relied on, other than what follows from the above.
Results may differ from a plain program's by a relative error of at most 0.0003.
Values sent between devices are 32-bit elements; how exact they have to be, the bound alone decides.
A program may use at most 128 MiB of HBM per device.

v0:
```python
import jax
import jax.numpy as jnp
from jax import lax
from jax.sharding import Mesh
from jax.sharding import PartitionSpec as P

ITERS = 3
ROW = ("row_0", "row_1")
COL = ("col_0", "col_1")
ROW_COL = ("row_0", "row_1", "col_0", "col_1")
exact_precision = lax.Precision.HIGHEST


def passed_along(shard, axis, by):
    peers = lax.axis_size(axis)
    pairs = [(i, i + by) for i in range(peers) if 0 <= i + by < peers]
    return lax.ppermute(shard, axis, pairs)


def with_halo(shard, sides, width):
    edges = {}
    for axis, dim in sides:
        peers, length = (lax.axis_size(axis), shard.shape[dim])
        up = [(i, (i + 1) % peers) for i in range(peers - 1)]
        last = lax.slice_in_dim(shard, length - width, length, axis=dim)
        first = lax.slice_in_dim(shard, 0, width, axis=dim)
        edges[dim] = (
            lax.ppermute(last, axis, up),
            lax.ppermute(first, axis, [(b, a) for a, b in up]),
        )
    done = []
    for _, dim in sides:
        low, high = edges[dim]
        around = [(width, width) if d in done else (0, 0) for d in range(shard.ndim)]
        shard = jnp.concatenate([jnp.pad(low, around), shard, jnp.pad(high, around)], axis=dim)
        done.append(dim)
    return shard


def one_axis_at_a_time(shard, axes):
    for axis in axes:
        shard = lax.psum(shard, axis)
    return shard


def neighbour_sum(padded, cond_x, cond_above, cond_y, cond_left):
    total = cond_x * padded[:, 2:, 1:-1] + cond_above * padded[:, :-2, 1:-1]
    return total + cond_y * padded[:, 1:-1, 2:] + cond_left * padded[:, 1:-1, :-2]


def gram(left, right):
    return jnp.einsum("kab,lab->kl", left, right, precision=exact_precision)


def combine(field, matrix):
    return jnp.einsum("kab,kl->lab", field, matrix, precision=exact_precision)


def small_solve(matrix, right):
    factor = jnp.linalg.cholesky(matrix)
    return jax.scipy.linalg.cho_solve((factor, True), right)


def shards(right_side, cond_x, cond_y, pad_mask):
    pad_nodes = pad_mask.astype(jnp.float32)
    free_nodes = 1.0 - pad_nodes
    upper_row = passed_along(cond_x[-1:], ROW, 1)
    cond_above = jnp.concatenate([upper_row, cond_x[:-1]], 0)
    left_column = passed_along(cond_y[:, -1:], COL, 1)
    cond_left = jnp.concatenate([left_column, cond_y[:, :-1]], 1)
    diagonal = free_nodes * (cond_x + cond_above + cond_y + cond_left) + pad_nodes
    inverse = 1.0 / diagonal
    solution = jnp.zeros_like(right_side)
    residual = right_side
    precond = residual * inverse
    direction = precond
    gram_now = one_axis_at_a_time(gram(residual, precond), ROW_COL)
    for iteration in range(ITERS):
        padded = with_halo(free_nodes * direction, ((ROW, 1), (COL, 2)), 1)
        image = pad_nodes * direction + free_nodes * (
            diagonal * direction - neighbour_sum(padded, cond_x, cond_above, cond_y, cond_left)
        )
        weighted = image * inverse
        curvature, cross_term, image_term = (
            one_axis_at_a_time(gram(direction, image), ROW_COL),
            one_axis_at_a_time(gram(image, precond), ROW_COL),
            one_axis_at_a_time(gram(image, weighted), ROW_COL),
        )
        alpha_block = small_solve(curvature, gram_now)
        solution = solution + combine(direction, alpha_block)
        residual = residual - combine(image, alpha_block)
        precond = residual * inverse
        mixed = jnp.dot(alpha_block.T, cross_term, precision=exact_precision)
        quadratic = jnp.dot(
            jnp.dot(alpha_block.T, image_term, precision=exact_precision),
            alpha_block,
            precision=exact_precision,
        )
        gram_next = gram_now - mixed - mixed.T + quadratic
        beta_block = small_solve(gram_now, gram_next)
        direction = precond + combine(direction, beta_block)
        gram_now = gram_next
    return (solution, residual)


def solution(mesh):
    split = Mesh(mesh.devices.reshape(4, 2, 4, 4), ("row_0", "row_1", "col_0", "col_1"))
    in_specs = (P(None, ROW, COL), P(ROW, COL), P(ROW, COL), P(ROW, COL))
    out_specs = (P(None, ROW, COL), P(None, ROW, COL))
    return jax.shard_map(
        shards, mesh=split, in_specs=in_specs, out_specs=out_specs, check_vma=False
    )
```

profile of v0, /device:TPU:8, one launch (start us, length us, event | category | flops | bytes accessed | tf_op | source)
XLA Modules:
  0.0 508.5 jit_solution(17853337915778137059)
XLA Ops:
  15.4 4.0 multiply_multiply_fusion
  38.3 30.3 %fusion.84 = f32[16,16]{0,1:T(8,128)S(1)} fusion(f32[16,256,384]{2,1,0:T(8,128)} %param.7, f32[256,384]{1,0:T(8,128)S(1)} %fusion.89), kind=kOutput, calls=%fused_computation.114 | convolution fusion | flops 303562752 | bytes 6685696 | tf_op jit(solution)/shard_map/kab,lab->kl/dot_general | solution.py:52
  73.4 20.2 %fusion.14 = f32[16,256,384]{2,0,1:T(8,128)S(1)} fusion(f32[16,256,1]{2,0,1:T(8,128)} %copy.33, f32[16,1,384]{2,0,1:T(8,128)S(1)} %collective-permute-done.2, f32[16,256,384]{2,0,1:T(8,128)} %copy-done.4, f32[16,1,384]{2,0,1:T(8,128)S(1)} %collective-permute-done.3, f32[16,256,1]{2,0,1:T(8,128)} %copy.31, f32[16,256,384]{2,1,0:T(8,128)} %param.7, ...), kind=kLoop, calls=%fused_computation.17 | loop fusion | flops 42467328 | bytes 22102016 | tf_op jit(solution)/shard_map/add | solution.py:80
  93.7 8.1 %fusion.78 = f32[16,16]{1,0:T(8,128)S(1)} fusion(f32[16,256,384]{2,0,1:T(8,128)S(1)} %fusion.14, f32[256,384]{1,0:T(8,128)S(1)} %fusion.89), kind=kOutput, calls=%fused_computation.105 | convolution fusion | flops 303562752 | bytes 6685696 | tf_op jit(solution)/shard_map/kab,lab->kl/dot_general | solution.py:52
  101.8 10.6 %fusion.75 = f32[16,16]{1,0:T(8,128)S(1)} fusion(f32[16,256,384]{2,0,1:T(8,128)S(1)} %fusion.14, f32[16,256,384]{2,1,0:T(8,128)S(1)} %bitcast.144, f32[256,384]{1,0:T(8,128)S(1)} %fusion.89), kind=kOutput, calls=%fused_computation.104 | convolution fusion | flops 303562752 | bytes 12977152 | tf_op jit(solution)/shard_map/kab,lab->kl/dot_general | solution.py:52
  112.4 10.6 %fusion.72 = f32[16,16]{0,1:T(8,128)S(1)} fusion(f32[16,256,384]{2,0,1:T(8,128)S(1)} %fusion.14, f32[16,256,384]{2,1,0:T(8,128)S(1)} %bitcast.144, f32[256,384]{1,0:T(8,128)S(1)} %fusion.89), kind=kOutput, calls=%fused_computation.103 | convolution fusion | flops 303562752 | bytes 12977152 | tf_op jit(solution)/shard_map/kab,lab->kl/dot_general | solution.py:52
  123.0 20.0 %all-reduce.11 = (f32[16,16]{0,1:T(8,128)S(1)}, f32[16,16]{0,1:T(8,128)S(1)}, f32[16,16]{1,0:T(8,128)S(1)}, f32[16,16]{1,0:T(8,128)S(1)}) all-reduce(f32[16,16]{0,1:T(8,128)S(1)} %fusion.84, f32[16,16]{0,1:T(8,128)S(1)} %fusion.72, f32[16,16]{1,0:T(8,128)S(1)} %fusion.78, ...), channel_id=1, replica_groups=mesh['row_0'=4,'row_1'=2,'col_0'=4,'col_1'=4] {'row_0'}, use_global_device_ids=true, to_apply=%region_6.8 | all-reduce | flops 1024 | bytes 8192 | tf_op jit(solution)/shard_map/psum | solution.py:42
  146.4 17.6 %all-reduce.9 = (f32[16,16]{0,1:T(8,128)S(1)}, f32[16,16]{0,1:T(8,128)S(1)}, f32[16,16]{1,0:T(8,128)S(1)}, f32[16,16]{1,0:T(8,128)S(1)}) all-reduce(f32[16,16]{0,1:T(8,128)S(1)} %get-tuple-element.32, f32[16,16]{0,1:T(8,128)S(1)} %get-tuple-element.33, ...), channel_id=1, replica_groups=mesh['row_0'=4,'row_1'=2,'col_0'=4,'col_1'=4] {'col_0'}, use_global_device_ids=true, to_apply=%region_8.10 | all-reduce | flops 1024 | bytes 8192 | tf_op jit(solution)/shard_map/psum | solution.py:42
  164.0 17.4 %all-reduce.7 = (f32[16,16]{0,1:T(8,128)S(1)}, f32[16,16]{0,1:T(8,128)S(1)}, f32[16,16]{1,0:T(8,128)S(1)}, f32[16,16]{1,0:T(8,128)S(1)}) all-reduce(f32[16,16]{0,1:T(8,128)S(1)} %get-tuple-element.18, f32[16,16]{0,1:T(8,128)S(1)} %get-tuple-element.19, ...), channel_id=1, replica_groups=mesh['row_0'=4,'row_1'=2,'col_0'=4,'col_1'=4] {'col_1'}, use_global_device_ids=true, to_apply=%region_9.11 | all-reduce | flops 1024 | bytes 8192 | tf_op jit(solution)/shard_map/psum | solution.py:42
  189.9 13.2 %copy_subtract_fusion = f32[16,256,384]{2,0,1:T(8,128)} fusion(f32[16,256,384]{2,1,0:T(8,128)} %param.7, f32[16,256,384]{2,0,1:T(8,128)} %copy-done.1, f32[16,16]{1,0:T(8,128)S(1)} %fusion.117), kind=kOutput, calls=%fused_computation.88 | convolution fusion | flops 303562752 | bytes 18875392 | tf_op jit(solution)/shard_map/kab,kl->lab/dot_general | solution.py:56
  204.3 15.0 %broadcast_multiply_fusion.1 = (f32[16,256,384]{2,0,1:T(8,128)S(1)}, f32[16,256,384]{2,0,1:T(8,128)}) fusion(f32[256,384]{1,0:T(8,128)S(1)} %get-tuple-element.52, f32[16,16,1]{0,1,2:T(8,128)S(1)} %convolution_bitcast_fusion.4, f32[16,256,384]{2,1,0:T(8,128)} %param.7, f32[256,384]{1,0:T(8,128)S(1)} %fusion.89, f32[16,256,384]{2,0,1:T(8,128)} %copy_subtract_fusion), kind=kOutput, calls=%fused_computation.91 | convolution fusion | flops 308281344 | bytes 25953280 | tf_op jit(solution)/shard_map/kab,kl->lab/dot_general | solution.py:56
  245.6 18.5 %fusion.34 = f32[16,256,384]{2,0,1:T(8,128)S(1)} fusion(f32[16,256,1]{2,0,1:T(8,128)} %copy.46, f32[16,1,384]{2,0,1:T(8,128)S(1)} %collective-permute-done.6, f32[16,256,384]{2,0,1:T(8,128)} %copy-done.5, f32[16,1,384]{2,0,1:T(8,128)S(1)} %collective-permute-done.7, f32[16,256,1]{2,0,1:T(8,128)} %copy.44, f32[16,256,384]{2,0,1:T(8,128)} %get-tuple-element.54, ...), kind=kLoop, calls=%fused_computation.46 | loop fusion | flops 40894464 | bytes 21708800 | tf_op jit(solution)/shard_map/add | solution.py:80
  264.1 8.1 %fusion.81 = f32[16,16]{1,0:T(8,128)S(1)} fusion(f32[16,256,384]{2,0,1:T(8,128)S(1)} %fusion.34, f32[256,384]{1,0:T(8,128)S(1)} %fusion.89), kind=kOutput, calls=%fused_computation.106 | convolution fusion | flops 303562752 | bytes 6685696 | tf_op jit(solution)/shard_map/kab,lab->kl/dot_general | solution.py:52
  272.3 8.1 %fusion.69 = f32[16,16]{1,0:T(8,128)S(1)} fusion(f32[16,256,384]{2,0,1:T(8,128)S(1)} %fusion.34, f32[16,256,384]{2,0,1:T(8,128)S(1)} %bitcast.150, f32[256,384]{1,0:T(8,128)S(1)} %fusion.89), kind=kOutput, calls=%fused_computation.102 | convolution fusion | flops 303562752 | bytes 12977152 | tf_op jit(solution)/shard_map/kab,lab->kl/dot_general | solution.py:52
  280.4 8.4 %convolution_bitcast_fusion.3 = f32[16,16]{0,1:T(8,128)S(1)} fusion(f32[16,256,384]{2,0,1:T(8,128)S(1)} %bitcast.148, f32[16,256,384]{2,0,1:T(8,128)S(1)} %fusion.34), kind=kOutput, calls=%fused_computation.111 | convolution fusion | flops 301989888 | bytes 12583936 | tf_op jit(solution)/shard_map/kab,lab->kl/dot_general | solution.py:52
  288.8 16.9 %all-reduce.10 = (f32[16,16]{0,1:T(8,128)S(1)}, f32[16,16]{1,0:T(8,128)S(1)}, f32[16,16]{1,0:T(8,128)S(1)}) all-reduce(f32[16,16]{0,1:T(8,128)S(1)} %convolution_bitcast_fusion.3, f32[16,16]{1,0:T(8,128)S(1)} %fusion.81, f32[16,16]{1,0:T(8,128)S(1)} %fusion.69), channel_id=1, replica_groups=mesh['row_0'=4,'row_1'=2,'col_0'=4,'col_1'=4] {'row_0'}, use_global_device_ids=true, to_apply=%region_18.21 | all-reduce | flops 768 | bytes 6144 | tf_op jit(solution)/shard_map/psum | solution.py:42
  309.1 14.4 %all-reduce.8 = (f32[16,16]{0,1:T(8,128)S(1)}, f32[16,16]{1,0:T(8,128)S(1)}, f32[16,16]{1,0:T(8,128)S(1)}) all-reduce(f32[16,16]{0,1:T(8,128)S(1)} %get-tuple-element.29, f32[16,16]{1,0:T(8,128)S(1)} %get-tuple-element.30, f32[16,16]{1,0:T(8,128)S(1)} %get-tuple-element.31), channel_id=1, replica_groups=mesh['row_0'=4,'row_1'=2,'col_0'=4,'col_1'=4] {'col_0'}, use_global_device_ids=true, to_apply=%region_20.23 | all-reduce | flops 768 | bytes 6144 | tf_op jit(solution)/shard_map/psum | solution.py:42
  323.5 17.4 %all-reduce.6 = (f32[16,16]{0,1:T(8,128)S(1)}, f32[16,16]{1,0:T(8,128)S(1)}, f32[16,16]{1,0:T(8,128)S(1)}) all-reduce(f32[16,16]{0,1:T(8,128)S(1)} %get-tuple-element.15, f32[16,16]{1,0:T(8,128)S(1)} %get-tuple-element.16, f32[16,16]{1,0:T(8,128)S(1)} %get-tuple-element.17), channel_id=1, replica_groups=mesh['row_0'=4,'row_1'=2,'col_0'=4,'col_1'=4] {'col_1'}, use_global_device_ids=true, to_apply=%region_21.24 | all-reduce | flops 768 | bytes 6144 | tf_op jit(solution)/shard_map/psum | solution.py:42
  345.3 10.7 %convolution_subtract_fusion.1 = f32[16,256,384]{2,0,1:T(8,128)} fusion(f32[16,256,384]{2,0,1:T(8,128)} %copy_subtract_fusion, f32[16,256,384]{2,0,1:T(8,128)} %copy-done.2, f32[16,16]{1,0:T(8,128)S(1)} %fusion.106), kind=kOutput, calls=%fused_computation.101 | convolution fusion | flops 303562752 | bytes 18875392 | tf_op jit(solution)/shard_map/kab,kl->lab/dot_general | solution.py:56
  357.1 11.0 %broadcast_multiply_fusion = (f32[16,256,384]{2,0,1:T(8,128)S(1)}, f32[16,256,384]{2,0,1:T(8,128)}) fusion(f32[256,384]{1,0:T(8,128)S(1)} %get-tuple-element.52, f32[16,16,1]{0,1,2:T(8,128)S(1)} %convolution_bitcast_fusion.2, f32[16,256,384]{2,0,1:T(8,128)} %get-tuple-element.54, f32[16,256,384]{2,0,1:T(8,128)} %convolution_subtract_fusion.1, ...), kind=kOutput, calls=%fused_computation.90 | convolution fusion | flops 306708480 | bytes 25953280 | tf_op jit(solution)/shard_map/kab,kl->lab/dot_general | solution.py:56
  378.9 4.9 collective-permute-start.13
  385.7 9.4 %fusion.104 = f32[16,256,384]{2,0,1:T(8,128)} fusion(f32[16,256,384]{2,0,1:T(8,128)} %get-tuple-element.54, f32[16,16]{1,0:T(8,128)S(1)} %fusion.106), kind=kOutput, calls=%fused_computation.143 | convolution fusion | flops 301989888 | bytes 12583936 | tf_op jit(solution)/shard_map/kab,kl->lab/dot_general | solution.py:56
  400.0 18.1 %fusion.22 = f32[16,256,384]{2,0,1:T(8,128)S(1)} fusion(f32[16,256,1]{2,0,1:T(8,128)} %copy.57, f32[16,1,384]{2,0,1:T(8,128)S(1)} %collective-permute-done.10, f32[16,256,384]{2,0,1:T(8,128)} %copy-done.6, f32[16,1,384]{2,0,1:T(8,128)S(1)} %collective-permute-done.11, f32[16,256,1]{2,0,1:T(8,128)} %copy.55, f32[16,256,384]{2,0,1:T(8,128)} %get-tuple-element.56, ...), kind=kLoop, calls=%fused_computation.26 | loop fusion | flops 40894464 | bytes 21708800 | tf_op jit(solution)/shard_map/add | solution.py:80
  420.8 10.2 %convolution_bitcast_fusion.1 = f32[16,16]{0,1:T(8,128)S(1)} fusion(f32[16,256,384]{2,0,1:T(8,128)} %get-tuple-element.56, f32[16,256,384]{2,0,1:T(8,128)S(1)} %fusion.22), kind=kOutput, calls=%fused_computation.108 | convolution fusion | flops 301989888 | bytes 12583936 | tf_op jit(solution)/shard_map/kab,lab->kl/dot_general | solution.py:52
  431.0 11.8 %psum.252 = f32[16,16]{0,1:T(8,128)S(1)} all-reduce(f32[16,16]{0,1:T(8,128)S(1)} %convolution_bitcast_fusion.1), channel_id=1, replica_groups=mesh['row_0'=4,'row_1'=2,'col_0'=4,'col_1'=4] {'row_0'}, use_global_device_ids=true, to_apply=%region_30.33 | all-reduce | flops 256 | bytes 2048 | tf_op jit(solution)/shard_map/psum | solution.py:42
  445.3 8.2 %psum.254 = f32[16,16]{0,1:T(8,128)S(1)} all-reduce(f32[16,16]{0,1:T(8,128)S(1)} %psum.253), channel_id=1, replica_groups=mesh['row_0'=4,'row_1'=2,'col_0'=4,'col_1'=4] {'col_0'}, use_global_device_ids=true, to_apply=%region_32.35 | all-reduce | flops 256 | bytes 2048 | tf_op jit(solution)/shard_map/psum | solution.py:42
  453.5 11.9 %psum.255 = f32[16,16]{0,1:T(8,128)S(1)} all-reduce(f32[16,16]{0,1:T(8,128)S(1)} %psum.254), channel_id=1, replica_groups=mesh['row_0'=4,'row_1'=2,'col_0'=4,'col_1'=4] {'col_1'}, use_global_device_ids=true, to_apply=%region_33.36 | all-reduce | flops 256 | bytes 2048 | tf_op jit(solution)/shard_map/psum | solution.py:42
  470.0 9.4 %convolution_subtract_fusion = f32[16,256,384]{2,0,1:T(8,128)S(1)} fusion(f32[16,256,384]{2,0,1:T(8,128)} %convolution_subtract_fusion.1, f32[16,16,1]{0,1,2:T(8,128)S(1)} %convolution_bitcast_fusion, f32[16,256,384]{2,0,1:T(8,128)} %copy-done.3), kind=kOutput, calls=%fused_computation.100 | convolution fusion | flops 303562752 | bytes 18875392 | tf_op jit(solution)/shard_map/kab,kl->lab/dot_general | solution.py:56
  479.4 7.6 %fusion.132 = f32[16,256,384]{2,0,1:T(8,128)S(1)} fusion(f32[16,16,1]{0,1,2:T(8,128)S(1)} %convolution_bitcast_fusion, f32[16,256,384]{2,0,1:T(8,128)} %get-tuple-element.56), kind=kOutput, calls=%fused_computation.187 | convolution fusion | flops 301989888 | bytes 12583936 | tf_op jit(solution)/shard_map/kab,kl->lab/dot_general | solution.py:56
  487.0 12.1 %add_add_fusion = f32[16,256,384]{2,0,1:T(8,128)S(1)} fusion(f32[16,256,384]{2,0,1:T(8,128)S(1)} %fusion.132, f32[16,256,384]{2,0,1:T(8,128)} %fusion.104, f32[16,256,384]{2,1,0:T(8,128)S(1)} %bitcast.146, f32[256,384]{1,0:T(8,128)S(1)} %fusion.89, f32[16,16]{1,0:T(8,128)S(1)} %fusion.117), kind=kOutput, calls=%fused_computation.80 | convolution fusion | flops 306708480 | bytes 25560064 | tf_op jit(solution)/shard_map/kab,kl->lab/dot_general | solution.py:56
  499.1 4.6 copy.62
  503.7 4.6 copy.63
  (151 shorter events, 113.6 us)
Async XLA Ops:
  0.6 14.8 %copy-start = (f32[16,256,384]{2,1,0:T(8,128)S(1)}, f32[16,256,384]{2,1,0:T(8,128)}, u32[]{:S(2)}) copy-start(f32[16,256,384]{2,1,0:T(8,128)} %param.7) | copy-start | bytes 18874372
  1.5 10.0 %collective-permute-start = (f32[1,384]{1,0:T(1,128)S(1)}, f32[1,384]{1,0:T(1,128)S(1)}, u32[]{:S(2)}, u32[]{:S(2)}) collective-permute-start(f32[1,384]{1,0:T(1,128)S(1)} %slice.108), channel_id=1, source_target_pairs={{0,16},{16,32},{32,48},{48,64},{64,80},{80,96},{96,112},{1,17},{17... | collective-permute-start | bytes 4616 | tf_op jit(solution)/shard_map/ppermute | solution.py:17
  4.5 7.0 %collective-permute-start.1 = (f32[256,1]{1,0:T(8,128)S(1)}, f32[256,1]{1,0:T(8,128)S(1)}, u32[]{:S(2)}, u32[]{:S(2)}) collective-permute-start(f32[256,1]{1,0:T(8,128)S(1)} %slice.110), channel_id=1, source_target_pairs={{0,1},{1,2},{2,3},{3,4},{4,5},{5,6},{6,7},{7,8},{8,9},{9,10},{10,1... | collective-permute-start | bytes 3080 | tf_op jit(solution)/shard_map/ppermute | solution.py:17
  19.5 2.7 copy-start.4
  24.2 49.2 %collective-permute-start.3 = (f32[16,1,384]{2,0,1:T(8,128)S(1)}, f32[16,1,384]{2,0,1:T(8,128)S(1)}, u32[]{:S(2)}, u32[]{:S(2)}) collective-permute-start(f32[16,1,384]{2,0,1:T(8,128)S(1)} %get-tuple-element.50), channel_id=1, source_target_pairs={{0,16},{16,32},{32,48},{48,64},{64,80},{80,96},{96,112},{1,17},{17... | collective-permute-start | bytes 73736 | tf_op jit(solution)/shard_map/ppermute | solution.py:28
  27.1 46.3 %collective-permute-start.2 = (f32[16,1,384]{2,0,1:T(8,128)S(1)}, f32[16,1,384]{2,0,1:T(8,128)S(1)}, u32[]{:S(2)}, u32[]{:S(2)}) collective-permute-start(f32[16,1,384]{2,0,1:T(8,128)S(1)} %get-tuple-element.51), channel_id=1, source_target_pairs={{16,0},{32,16},{48,32},{64,48},{80,64},{96,80},{112,96},{17,1},{33... | collective-permute-start | bytes 73736 | tf_op jit(solution)/shard_map/ppermute | solution.py:29
  32.0 41.4 %copy-start.7 = (f32[256,384]{1,0:T(8,128)S(1)}, f32[256,384]{1,0:T(8,128)}, u32[]{:S(2)}) copy-start(f32[256,384]{1,0:T(8,128)} %param.9) | copy-start | bytes 1179652
  32.0 39.0 %collective-permute-start.5 = (f32[16,256,1]{1,0,2:T(8,128)S(1)}, f32[16,256,1]{1,0,2:T(8,128)S(1)}, u32[]{:S(2)}, u32[]{:S(2)}) collective-permute-start(f32[16,256,1]{1,0,2:T(8,128)S(1)} %copy.32), channel_id=1, source_target_pairs={{0,1},{1,2},{2,3},{3,4},{4,5},{5,6},{6,7},{7,8},{8,9},{9,10},{10,1... | collective-permute-start | bytes 49160 | tf_op jit(solution)/shard_map/ppermute | solution.py:28
  35.6 33.0 %collective-permute-start.4 = (f32[16,256,1]{1,0,2:T(8,128)S(1)}, f32[16,256,1]{1,0,2:T(8,128)S(1)}, u32[]{:S(2)}, u32[]{:S(2)}) collective-permute-start(f32[16,256,1]{1,0,2:T(8,128)S(1)} %copy.30), channel_id=1, source_target_pairs={{1,0},{2,1},{3,2},{4,3},{5,4},{6,5},{7,6},{8,7},{9,8},{10,9},{11,1... | collective-permute-start | bytes 49160 | tf_op jit(solution)/shard_map/ppermute | solution.py:29
  71.0 30.8 %slice-start = ((s8[6291456]{0:T(1024)(128)(4,1)}), s8[2097152]{0:T(1024)(128)(4,1)S(1)}, s32[]{:S(2)}) async-start(s8[6291456]{0:T(1024)(128)(4,1)} %bitcast.143), calls=%async_computation | async-start | bytes 4194304
  73.4 28.4 %slice-start.1 = ((s8[6291456]{0:T(1024)(128)(4,1)}), s8[4194304]{0:T(1024)(128)(4,1)S(1)}, s32[]{:S(2)}) async-start(s8[6291456]{0:T(1024)(128)(4,1)} %bitcast.143), calls=%async_computation.1 | async-start | bytes 8388608
  93.7 18.8 %copy-start.1 = (f32[16,256,384]{2,0,1:T(8,128)}, f32[16,256,384]{2,0,1:T(8,128)S(1)}, u32[]{:S(2)}) copy-start(f32[16,256,384]{2,0,1:T(8,128)S(1)} %fusion.14) | copy-start | bytes 18874372
  226.1 19.4 %collective-permute-start.7 = (f32[16,1,384]{2,0,1:T(8,128)S(1)}, f32[16,1,384]{2,0,1:T(8,128)S(1)}, u32[]{:S(2)}, u32[]{:S(2)}) collective-permute-start(f32[16,1,384]{2,0,1:T(8,128)S(1)} %get-tuple-element.46), channel_id=1, source_target_pairs={{0,16},{16,32},{32,48},{48,64},{64,80},{80,96},{96,112},{1,17},{17... | collective-permute-start | bytes 73736 | tf_op jit(solution)/shard_map/ppermute | solution.py:28
  227.4 18.2 %collective-permute-start.6 = (f32[16,1,384]{2,0,1:T(8,128)S(1)}, f32[16,1,384]{2,0,1:T(8,128)S(1)}, u32[]{:S(2)}, u32[]{:S(2)}) collective-permute-start(f32[16,1,384]{2,0,1:T(8,128)S(1)} %get-tuple-element.47), channel_id=1, source_target_pairs={{16,0},{32,16},{48,32},{64,48},{80,64},{96,80},{112,96},{17,1},{33... | collective-permute-start | bytes 73736 | tf_op jit(solution)/shard_map/ppermute | solution.py:29
  232.3 10.9 %collective-permute-start.9 = (f32[16,256,1]{1,0,2:T(8,128)S(1)}, f32[16,256,1]{1,0,2:T(8,128)S(1)}, u32[]{:S(2)}, u32[]{:S(2)}) collective-permute-start(f32[16,256,1]{1,0,2:T(8,128)S(1)} %copy.45), channel_id=1, source_target_pairs={{0,1},{1,2},{2,3},{3,4},{4,5},{5,6},{6,7},{7,8},{8,9},{9,10},{10,1... | collective-permute-start | bytes 49160 | tf_op jit(solution)/shard_map/ppermute | solution.py:28
  234.9 5.8 %collective-permute-start.8 = (f32[16,256,1]{1,0,2:T(8,128)S(1)}, f32[16,256,1]{1,0,2:T(8,128)S(1)}, u32[]{:S(2)}, u32[]{:S(2)}) collective-permute-start(f32[16,256,1]{1,0,2:T(8,128)S(1)} %copy.43), channel_id=1, source_target_pairs={{1,0},{2,1},{3,2},{4,3},{5,4},{6,5},{7,6},{8,7},{9,8},{10,9},{11,1... | collective-permute-start | bytes 49160 | tf_op jit(solution)/shard_map/ppermute | solution.py:29
  243.2 29.1 %slice-start.6 = ((s8[6291456]{0:T(1024)(128)(4,1)}), s8[2097152]{0:T(1024)(128)(4,1)S(1)}, s32[]{:S(2)}) async-start(s8[6291456]{0:T(1024)(128)(4,1)} %bitcast.149), calls=%async_computation.6 | async-start | bytes 4194304
  245.6 26.7 %slice-start.7 = ((s8[6291456]{0:T(1024)(128)(4,1)}), s8[4194304]{0:T(1024)(128)(4,1)S(1)}, s32[]{:S(2)}) async-start(s8[6291456]{0:T(1024)(128)(4,1)} %bitcast.149), calls=%async_computation.7 | async-start | bytes 8388608
  264.1 16.2 %copy-start.2 = (f32[16,256,384]{2,0,1:T(8,128)}, f32[16,256,384]{2,0,1:T(8,128)S(1)}, u32[]{:S(2)}) copy-start(f32[16,256,384]{2,0,1:T(8,128)S(1)} %fusion.34) | copy-start | bytes 18874372
  264.1 16.2 %slice-start.4 = ((s8[6291456]{0:T(1024)(128)(4,1)}), s8[4194304]{0:T(1024)(128)(4,1)S(1)}, s32[]{:S(2)}) async-start(s8[6291456]{0:T(1024)(128)(4,1)} %bitcast.147), calls=%async_computation.4 | async-start | bytes 8388608
  272.2 8.1 %slice-start.5 = ((s8[6291456]{0:T(1024)(128)(4,1)}), s8[2097152]{0:T(1024)(128)(4,1)S(1)}, s32[]{:S(2)}) async-start(s8[6291456]{0:T(1024)(128)(4,1)} %bitcast.147), calls=%async_computation.5 | async-start | bytes 4194304
  372.7 27.2 %collective-permute-start.11 = (f32[16,1,384]{2,0,1:T(8,128)S(1)}, f32[16,1,384]{2,0,1:T(8,128)S(1)}, u32[]{:S(2)}, u32[]{:S(2)}) collective-permute-start(f32[16,1,384]{2,0,1:T(8,128)S(1)} %get-tuple-element.42), channel_id=1, source_target_pairs={{0,16},{16,32},{32,48},{48,64},{64,80},{80,96},{96,112},{1,17},{17... | collective-permute-start | bytes 73736 | tf_op jit(solution)/shard_map/ppermute | solution.py:28
  374.0 25.9 %collective-permute-start.10 = (f32[16,1,384]{2,0,1:T(8,128)S(1)}, f32[16,1,384]{2,0,1:T(8,128)S(1)}, u32[]{:S(2)}, u32[]{:S(2)}) collective-permute-start(f32[16,1,384]{2,0,1:T(8,128)S(1)} %get-tuple-element.43), channel_id=1, source_target_pairs={{16,0},{32,16},{48,32},{64,48},{80,64},{96,80},{112,96},{17,1},{33... | collective-permute-start | bytes 73736 | tf_op jit(solution)/shard_map/ppermute | solution.py:29
  378.9 21.1 %copy-start.8 = (f32[256,384]{1,0:T(8,128)S(1)}, f32[256,384]{1,0:T(8,128)}, u32[]{:S(2)}) copy-start(f32[256,384]{1,0:T(8,128)} %param.8) | copy-start | bytes 1179652
  378.9 21.1 %copy-start.9 = (f32[256,384]{1,0:T(8,128)S(1)}, f32[256,384]{1,0:T(8,128)}, u32[]{:S(2)}) copy-start(f32[256,384]{1,0:T(8,128)} %convert_element_type.10) | copy-start | bytes 1179652
  378.9 21.1 %copy-start.10 = (f32[256,384]{1,0:T(8,128)S(1)}, f32[256,384]{1,0:T(8,128)}, u32[]{:S(2)}) copy-start(f32[256,384]{1,0:T(8,128)} %get-tuple-element.36) | copy-start | bytes 1179652
  378.9 21.1 %copy-start.11 = (f32[256,384]{1,0:T(8,128)S(1)}, f32[256,384]{1,0:T(8,128)}, u32[]{:S(2)}) copy-start(f32[256,384]{1,0:T(8,128)} %get-tuple-element.38) | copy-start | bytes 1179652
  378.9 21.1 %copy-start.12 = (f32[256,384]{1,0:T(8,128)S(1)}, f32[256,384]{1,0:T(8,128)}, u32[]{:S(2)}) copy-start(f32[256,384]{1,0:T(8,128)} %get-tuple-element.39) | copy-start | bytes 1179652
  378.9 18.7 %collective-permute-start.13 = (f32[16,256,1]{1,0,2:T(8,128)S(1)}, f32[16,256,1]{1,0,2:T(8,128)S(1)}, u32[]{:S(2)}, u32[]{:S(2)}) collective-permute-start(f32[16,256,1]{1,0,2:T(8,128)S(1)} %copy.56), channel_id=1, source_target_pairs={{0,1},{1,2},{2,3},{3,4},{4,5},{5,6},{6,7},{7,8},{8,9},{9,10},{10,1... | collective-permute-start | bytes 49160 | tf_op jit(solution)/shard_map/ppermute | solution.py:28
  383.8 11.4 %collective-permute-start.12 = (f32[16,256,1]{1,0,2:T(8,128)S(1)}, f32[16,256,1]{1,0,2:T(8,128)S(1)}, u32[]{:S(2)}, u32[]{:S(2)}) collective-permute-start(f32[16,256,1]{1,0,2:T(8,128)S(1)} %copy.54), channel_id=1, source_target_pairs={{1,0},{2,1},{3,2},{4,3},{5,4},{6,5},{7,6},{8,7},{9,8},{10,9},{11,1... | collective-permute-start | bytes 49160 | tf_op jit(solution)/shard_map/ppermute | solution.py:29
  420.8 66.2 %slice-start.2 = ((s8[6291456]{0:T(1024)(128)(4,1)}), s8[2097152]{0:T(1024)(128)(4,1)S(1)}, s32[]{:S(2)}) async-start(s8[6291456]{0:T(1024)(128)(4,1)} %bitcast.145), calls=%async_computation.2 | async-start | bytes 4194304
  470.0 17.0 %slice-start.3 = ((s8[6291456]{0:T(1024)(128)(4,1)}), s8[4194304]{0:T(1024)(128)(4,1)S(1)}, s32[]{:S(2)}) async-start(s8[6291456]{0:T(1024)(128)(4,1)} %bitcast.145), calls=%async_computation.3 | async-start | bytes 8388608
  (3 other events, 8.0 us)
where the time goes:
time: 515 us; the launch traced here: 509 us
  matrix products  186 us (36%)
  blocking collectives  145 us (28%)
  other arithmetic  86.4 us (17%)
  local copies, waits for them, and re-layouts  53.4 us (10%)
  starting transfers between devices  33.9 us (7%)
    psum x12, blocking collectives, one_axis_at_a_time(): shard = lax.psum(shard, axis)  145 us
    dot_general x8, matrix products, gram(): return jnp.einsum('kab,lab->kl', left, right, precision=exact_precision)  94.3 us
    dot_general x8, matrix products, combine(): return jnp.einsum('kab,kl->lab', field, matrix, precision=exact_precision)  88.5 us
    add x3, other arithmetic, shards(): pad_nodes * direction  56.9 us
    unnamed x44, local copies, waits for them, and re-layouts  20 us
    ppermute x6, starting transfers between devices, with_halo(): lax.ppermute(last, axis, up)  16.7 us
    slice x6, local copies, waits for them, and re-layouts, with_halo(): first = lax.slice_in_dim(shard, 0, width, axis=dim)  13.6 us
    ppermute x6, starting transfers between devices, with_halo(): lax.ppermute(first, axis, [(b, a) for a, b in up])  11.7 us
  transfers between devices with their start and end apart: 14, of which 2 were waited for; matrix products, arithmetic and copies ran while one was open for 14% of the time, Pallas kernels for 0%

commit v1 on v0

--- a/solution.py
+++ b/solution.py
@@ -39,7 +39,7 @@
 
 def one_axis_at_a_time(shard, axes):
     for axis in axes:
-        shard = lax.psum(shard, axis)
+        shard = jnp.sum(lax.all_gather(shard, axis), axis=0)
     return shard
 
 

time: 515 us -> 669 us (1.30)
  blocking collectives: 145 us -> 316 us
  matrix products: 186 us -> 168 us
    all_gather x0 -> x32, blocking collectives: none -> 316 us  [one_axis_at_a_time(): shard = jnp.sum(lax.all_gather(shard, axis), axis=0)]
    psum x12 -> x0, blocking collectives: 145 us -> none  [one_axis_at_a_time(): shard = lax.psum(shard, axis)]
    dot_general x8, matrix products: 94.3 us -> 76.2 us  [gram(): return jnp.einsum('kab,lab->kl', left, right, precision=exact_precision)]
  transfers between devices with their start and end apart: 14 -> 14, of which waited for: 2 -> 3; matrix products, arithmetic and copies ran while one was open for 14% -> 6% of each run, Pallas kernels for 0% -> 0%
where the time goes in v1:
time: 669 us; the launch traced here: 658 us
  blocking collectives  316 us (47%)
  matrix products  168 us (25%)
  other arithmetic  87.3 us (13%)
  local copies, waits for them, and re-layouts  50.8 us (8%)
  starting transfers between devices  30.8 us (5%)
    all_gather x32, blocking collectives, one_axis_at_a_time(): shard = jnp.sum(lax.all_gather(shard, axis), axis=0)  316 us
    dot_general x8, matrix products, combine(): return jnp.einsum('kab,kl->lab', field, matrix, precision=exact_precision)  88.5 us
    dot_general x8, matrix products, gram(): return jnp.einsum('kab,lab->kl', left, right, precision=exact_precision)  76.2 us
    add x3, other arithmetic, shards(): pad_nodes * direction  57.1 us
    unnamed x44, local copies, waits for them, and re-layouts  17.3 us
    ppermute x6, starting transfers between devices, with_halo(): lax.ppermute(first, axis, [(b, a) for a, b in up])  13.9 us
    slice x6, local copies, waits for them, and re-layouts, with_halo(): first = lax.slice_in_dim(shard, 0, width, axis=dim)  13.6 us
  transfers between devices with their start and end apart: 14, of which 3 were waited for; matrix products, arithmetic and copies ran while one was open for 6% of the time, Pallas kernels for 0%

profile of v1, /device:TPU:8, one launch (start us, length us, event | category | flops | bytes accessed | tf_op | source)
XLA Modules:
  0.0 658.3 jit_solution(756020658558548414)
XLA Ops:
  34.6 13.9 %all-gather.4 = f32[64,16]{1,0:T(8,128)S(1)} all-gather(f32[16,16]{1,0:T(8,128)S(1)} %copy.228), channel_id=6, replica_groups=mesh['row_0'=4,'row_1'=2,'col_0'=4,'col_1'=4] {'row_0'}, dimensions={0}, use_global_device_ids=true | all-gather | bytes 5120 | tf_op jit(solution)/shard_map/all_gather | solution.py:42
  50.3 12.3 %all-gather.6 = f32[64,16]{1,0:T(8,128)S(1)} all-gather(f32[16,16]{1,0:T(8,128)S(1)} %reduce_sum.293), channel_id=8, replica_groups=mesh['row_0'=4,'row_1'=2,'col_0'=4,'col_1'=4] {'col_0'}, dimensions={0}, use_global_device_ids=true | all-gather | bytes 5120 | tf_op jit(solution)/shard_map/all_gather | solution.py:42
  62.6 12.1 %all-gather.7 = f32[64,16]{1,0:T(8,128)S(1)} all-gather(f32[16,16]{1,0:T(8,128)S(1)} %reduce_sum.294), channel_id=9, replica_groups=mesh['row_0'=4,'row_1'=2,'col_0'=4,'col_1'=4] {'col_1'}, dimensions={0}, use_global_device_ids=true | all-gather | bytes 5120 | tf_op jit(solution)/shard_map/all_gather | solution.py:42
  97.3 20.5 %fusion.14 = f32[16,256,384]{2,0,1:T(8,128)S(1)} fusion(f32[16,256,1]{2,0,1:T(8,128)} %copy.225, f32[16,1,384]{2,0,1:T(8,128)S(1)} %collective-permute-done.2, f32[16,256,384]{2,0,1:T(8,128)} %copy-done.4, f32[16,1,384]{2,0,1:T(8,128)S(1)} %collective-permute-done.3, f32[16,256,1]{2,0,1:T(8,128)} %copy.223, f32[16,256,384]{2,1,0:T(8,128)} %param.7, ...), kind=kLoop, calls=%fused_computation.17 | loop fusion | flops 42467328 | bytes 22102016 | tf_op jit(solution)/shard_map/add | solution.py:80
  147.0 13.9 %all-gather = f32[64,16]{1,0:T(8,128)S(1)} all-gather(f32[16,16]{1,0:T(8,128)S(1)} %fusion.72), channel_id=2, replica_groups=mesh['row_0'=4,'row_1'=2,'col_0'=4,'col_1'=4] {'row_0'}, dimensions={0}, use_global_device_ids=true | all-gather | bytes 5120 | tf_op jit(solution)/shard_map/all_gather | solution.py:42
  162.8 11.9 %all-gather.2 = f32[64,16]{1,0:T(8,128)S(1)} all-gather(f32[16,16]{1,0:T(8,128)S(1)} %reduce_sum.289), channel_id=4, replica_groups=mesh['row_0'=4,'row_1'=2,'col_0'=4,'col_1'=4] {'col_0'}, dimensions={0}, use_global_device_ids=true | all-gather | bytes 5120 | tf_op jit(solution)/shard_map/all_gather | solution.py:42
  174.7 15.5 %all-gather.3 = f32[64,16]{1,0:T(8,128)S(1)} all-gather(f32[16,16]{1,0:T(8,128)S(1)} %reduce_sum.290), channel_id=5, replica_groups=mesh['row_0'=4,'row_1'=2,'col_0'=4,'col_1'=4] {'col_1'}, dimensions={0}, use_global_device_ids=true | all-gather | bytes 5120 | tf_op jit(solution)/shard_map/all_gather | solution.py:42
  194.6 13.2 %copy_subtract_fusion = f32[16,256,384]{2,0,1:T(8,128)} fusion(f32[16,256,384]{2,1,0:T(8,128)} %param.7, f32[16,256,384]{2,0,1:T(8,128)} %copy-done.1, f32[16,16]{1,0:T(8,128)S(1)} %fusion.117), kind=kOutput, calls=%fused_computation.88 | convolution fusion | flops 303562752 | bytes 18875392 | tf_op jit(solution)/shard_map/kab,kl->lab/dot_general | solution.py:56
  207.8 11.9 %all-gather.8 = f32[64,16]{1,0:T(8,128)S(1)} all-gather(f32[16,16]{1,0:T(8,128)S(1)} %fusion.75), channel_id=10, replica_groups=mesh['row_0'=4,'row_1'=2,'col_0'=4,'col_1'=4] {'row_0'}, dimensions={0}, use_global_device_ids=true | all-gather | bytes 5120 | tf_op jit(solution)/shard_map/all_gather | solution.py:42
  221.6 11.9 %all-gather.10 = f32[64,16]{1,0:T(8,128)S(1)} all-gather(f32[16,16]{1,0:T(8,128)S(1)} %reduce_sum.297), channel_id=12, replica_groups=mesh['row_0'=4,'row_1'=2,'col_0'=4,'col_1'=4] {'col_0'}, dimensions={0}, use_global_device_ids=true | all-gather | bytes 5120 | tf_op jit(solution)/shard_map/all_gather | solution.py:42
  233.5 11.9 %all-gather.11 = f32[64,16]{1,0:T(8,128)S(1)} all-gather(f32[16,16]{1,0:T(8,128)S(1)} %reduce_sum.298), channel_id=13, replica_groups=mesh['row_0'=4,'row_1'=2,'col_0'=4,'col_1'=4] {'col_1'}, dimensions={0}, use_global_device_ids=true | all-gather | bytes 5120 | tf_op jit(solution)/shard_map/all_gather | solution.py:42
  245.7 11.9 %all-gather.12 = f32[64,16]{1,0:T(8,128)S(1)} all-gather(f32[16,16]{1,0:T(8,128)S(1)} %fusion.78), channel_id=14, replica_groups=mesh['row_0'=4,'row_1'=2,'col_0'=4,'col_1'=4] {'row_0'}, dimensions={0}, use_global_device_ids=true | all-gather | bytes 5120 | tf_op jit(solution)/shard_map/all_gather | solution.py:42
  259.5 11.9 %all-gather.14 = f32[64,16]{1,0:T(8,128)S(1)} all-gather(f32[16,16]{1,0:T(8,128)S(1)} %reduce_sum.301), channel_id=16, replica_groups=mesh['row_0'=4,'row_1'=2,'col_0'=4,'col_1'=4] {'col_0'}, dimensions={0}, use_global_device_ids=true | all-gather | bytes 5120 | tf_op jit(solution)/shard_map/all_gather | solution.py:42
  271.4 11.9 %all-gather.15 = f32[64,16]{1,0:T(8,128)S(1)} all-gather(f32[16,16]{1,0:T(8,128)S(1)} %reduce_sum.302), channel_id=17, replica_groups=mesh['row_0'=4,'row_1'=2,'col_0'=4,'col_1'=4] {'col_1'}, dimensions={0}, use_global_device_ids=true | all-gather | bytes 5120 | tf_op jit(solution)/shard_map/all_gather | solution.py:42
  284.2 15.0 %broadcast_multiply_fusion.1 = (f32[16,256,384]{2,0,1:T(8,128)S(1)}, f32[16,256,384]{2,0,1:T(8,128)}) fusion(f32[256,384]{1,0:T(8,128)S(1)} %get-tuple-element.34, f32[16,16,1]{0,1,2:T(8,128)S(1)} %convolution_bitcast_fusion.4, f32[16,256,384]{2,1,0:T(8,128)} %param.7, f32[256,384]{1,0:T(8,128)S(1)} %fusion.89, f32[16,256,384]{2,0,1:T(8,128)} %copy_subtract_fusion), kind=kOutput, calls=%fused_computation.91 | convolution fusion | flops 308281344 | bytes 25953280 | tf_op jit(solution)/shard_map/kab,kl->lab/dot_general | solution.py:56
  325.2 18.5 %fusion.34 = f32[16,256,384]{2,0,1:T(8,128)S(1)} fusion(f32[16,256,1]{2,0,1:T(8,128)} %copy.246, f32[16,1,384]{2,0,1:T(8,128)S(1)} %collective-permute-done.6, f32[16,256,384]{2,0,1:T(8,128)} %copy-done.5, f32[16,1,384]{2,0,1:T(8,128)S(1)} %collective-permute-done.7, f32[16,256,1]{2,0,1:T(8,128)} %copy.244, f32[16,256,384]{2,0,1:T(8,128)} %get-tuple-element.36, ...), kind=kLoop, calls=%fused_computation.46 | loop fusion | flops 40894464 | bytes 21708800 | tf_op jit(solution)/shard_map/add | solution.py:80
  368.3 14.9 %all-gather.16 = f32[64,16]{1,0:T(8,128)S(1)} all-gather(f32[16,16]{1,0:T(8,128)S(1)} %convolution_bitcast_fusion.3), channel_id=18, replica_groups=mesh['row_0'=4,'row_1'=2,'col_0'=4,'col_1'=4] {'row_0'}, dimensions={0}, use_global_device_ids=true | all-gather | bytes 5120 | tf_op jit(solution)/shard_map/all_gather | solution.py:42
  385.1 11.9 %all-gather.18 = f32[64,16]{1,0:T(8,128)S(1)} all-gather(f32[16,16]{1,0:T(8,128)S(1)} %reduce_sum.305), channel_id=20, replica_groups=mesh['row_0'=4,'row_1'=2,'col_0'=4,'col_1'=4] {'col_0'}, dimensions={0}, use_global_device_ids=true | all-gather | bytes 5120 | tf_op jit(solution)/shard_map/all_gather | solution.py:42
  397.0 13.7 %all-gather.19 = f32[64,16]{1,0:T(8,128)S(1)} all-gather(f32[16,16]{1,0:T(8,128)S(1)} %reduce_sum.306), channel_id=21, replica_groups=mesh['row_0'=4,'row_1'=2,'col_0'=4,'col_1'=4] {'col_1'}, dimensions={0}, use_global_device_ids=true | all-gather | bytes 5120 | tf_op jit(solution)/shard_map/all_gather | solution.py:42
  425.8 11.9 %all-gather.20 = f32[64,16]{1,0:T(8,128)S(1)} all-gather(f32[16,16]{1,0:T(8,128)S(1)} %fusion.69), channel_id=22, replica_groups=mesh['row_0'=4,'row_1'=2,'col_0'=4,'col_1'=4] {'row_0'}, dimensions={0}, use_global_device_ids=true | all-gather | bytes 5120 | tf_op jit(solution)/shard_map/all_gather | solution.py:42
  439.5 11.9 %all-gather.22 = f32[64,16]{1,0:T(8,128)S(1)} all-gather(f32[16,16]{1,0:T(8,128)S(1)} %reduce_sum.309), channel_id=24, replica_groups=mesh['row_0'=4,'row_1'=2,'col_0'=4,'col_1'=4] {'col_0'}, dimensions={0}, use_global_device_ids=true | all-gather | bytes 5120 | tf_op jit(solution)/shard_map/all_gather | solution.py:42
  451.4 11.9 %all-gather.23 = f32[64,16]{1,0:T(8,128)S(1)} all-gather(f32[16,16]{1,0:T(8,128)S(1)} %reduce_sum.310), channel_id=25, replica_groups=mesh['row_0'=4,'row_1'=2,'col_0'=4,'col_1'=4] {'col_1'}, dimensions={0}, use_global_device_ids=true | all-gather | bytes 5120 | tf_op jit(solution)/shard_map/all_gather | solution.py:42
  463.6 11.9 %all-gather.24 = f32[64,16]{1,0:T(8,128)S(1)} all-gather(f32[16,16]{1,0:T(8,128)S(1)} %fusion.81), channel_id=26, replica_groups=mesh['row_0'=4,'row_1'=2,'col_0'=4,'col_1'=4] {'row_0'}, dimensions={0}, use_global_device_ids=true | all-gather | bytes 5120 | tf_op jit(solution)/shard_map/all_gather | solution.py:42
  477.4 11.9 %all-gather.26 = f32[64,16]{1,0:T(8,128)S(1)} all-gather(f32[16,16]{1,0:T(8,128)S(1)} %reduce_sum.313), channel_id=28, replica_groups=mesh['row_0'=4,'row_1'=2,'col_0'=4,'col_1'=4] {'col_0'}, dimensions={0}, use_global_device_ids=true | all-gather | bytes 5120 | tf_op jit(solution)/shard_map/all_gather | solution.py:42
  489.4 11.9 %all-gather.27 = f32[64,16]{1,0:T(8,128)S(1)} all-gather(f32[16,16]{1,0:T(8,128)S(1)} %reduce_sum.314), channel_id=29, replica_groups=mesh['row_0'=4,'row_1'=2,'col_0'=4,'col_1'=4] {'col_1'}, dimensions={0}, use_global_device_ids=true | all-gather | bytes 5120 | tf_op jit(solution)/shard_map/all_gather | solution.py:42
  502.1 11.0 %broadcast_multiply_fusion = (f32[16,256,384]{2,0,1:T(8,128)S(1)}, f32[16,256,384]{2,0,1:T(8,128)}) fusion(f32[256,384]{1,0:T(8,128)S(1)} %get-tuple-element.34, f32[16,16,1]{0,1,2:T(8,128)S(1)} %convolution_bitcast_fusion.2, f32[16,256,384]{2,0,1:T(8,128)} %get-tuple-element.36, f32[16,256,384]{2,0,1:T(8,128)} %convolution_subtract_fusion.1, ...), kind=kOutput, calls=%fused_computation.90 | convolution fusion | flops 306708480 | bytes 25953280 | tf_op jit(solution)/shard_map/kab,kl->lab/dot_general | solution.py:56
  544.1 18.1 %fusion.22 = f32[16,256,384]{2,0,1:T(8,128)S(1)} fusion(f32[16,256,1]{2,0,1:T(8,128)} %copy.257, f32[16,1,384]{2,0,1:T(8,128)S(1)} %collective-permute-done.10, f32[16,256,384]{2,0,1:T(8,128)} %copy-done.6, f32[16,1,384]{2,0,1:T(8,128)S(1)} %collective-permute-done.11, f32[16,256,1]{2,0,1:T(8,128)} %copy.255, f32[16,256,384]{2,0,1:T(8,128)} %get-tuple-element.38, ...), kind=kLoop, calls=%fused_computation.26 | loop fusion | flops 40894464 | bytes 21708800 | tf_op jit(solution)/shard_map/add | solution.py:80
  562.2 12.3 %convolution_bitcast_fusion.1 = f32[16,16]{1,0:T(8,128)S(1)} fusion(f32[16,256,384]{2,0,1:T(8,128)} %get-tuple-element.38, f32[16,256,384]{2,0,1:T(8,128)S(1)} %fusion.22), kind=kOutput, calls=%fused_computation.108 | convolution fusion | flops 301989888 | bytes 12583936 | tf_op jit(solution)/shard_map/kab,lab->kl/dot_general | solution.py:52
  574.6 14.9 %all-gather.28 = f32[64,16]{1,0:T(8,128)S(1)} all-gather(f32[16,16]{1,0:T(8,128)S(1)} %convolution_bitcast_fusion.1), channel_id=30, replica_groups=mesh['row_0'=4,'row_1'=2,'col_0'=4,'col_1'=4] {'row_0'}, dimensions={0}, use_global_device_ids=true | all-gather | bytes 5120 | tf_op jit(solution)/shard_map/all_gather | solution.py:42
  591.3 11.9 %all-gather.30 = f32[64,16]{1,0:T(8,128)S(1)} all-gather(f32[16,16]{1,0:T(8,128)S(1)} %reduce_sum.317), channel_id=32, replica_groups=mesh['row_0'=4,'row_1'=2,'col_0'=4,'col_1'=4] {'col_0'}, dimensions={0}, use_global_device_ids=true | all-gather | bytes 5120 | tf_op jit(solution)/shard_map/all_gather | solution.py:42
  603.2 12.0 %all-gather.31 = f32[64,16]{1,0:T(8,128)S(1)} all-gather(f32[16,16]{1,0:T(8,128)S(1)} %reduce_sum.318), channel_id=33, replica_groups=mesh['row_0'=4,'row_1'=2,'col_0'=4,'col_1'=4] {'col_1'}, dimensions={0}, use_global_device_ids=true | all-gather | bytes 5120 | tf_op jit(solution)/shard_map/all_gather | solution.py:42
  636.8 12.1 %add_add_fusion = f32[16,256,384]{2,0,1:T(8,128)S(1)} fusion(f32[16,256,384]{2,0,1:T(8,128)S(1)} %fusion.132, f32[16,256,384]{2,0,1:T(8,128)} %fusion.104, f32[16,256,384]{2,1,0:T(8,128)S(1)} %bitcast.178, f32[256,384]{1,0:T(8,128)S(1)} %fusion.89, f32[16,16]{1,0:T(8,128)S(1)} %fusion.117), kind=kOutput, calls=%fused_computation.80 | convolution fusion | flops 306708480 | bytes 25560064 | tf_op jit(solution)/shard_map/kab,kl->lab/dot_general | solution.py:56
  (205 shorter events, 234.2 us)
Async XLA Ops:
  0.6 14.8 %copy-start = (f32[16,256,384]{2,1,0:T(8,128)S(1)}, f32[16,256,384]{2,1,0:T(8,128)}, u32[]{:S(2)}) copy-start(f32[16,256,384]{2,1,0:T(8,128)} %param.7) | copy-start | bytes 18874372
  1.5 10.0 %collective-permute-start = (f32[1,384]{1,0:T(1,128)S(1)}, f32[1,384]{1,0:T(1,128)S(1)}, u32[]{:S(2)}, u32[]{:S(2)}) collective-permute-start(f32[1,384]{1,0:T(1,128)S(1)} %slice.108), channel_id=1, source_target_pairs={{0,16},{16,32},{32,48},{48,64},{64,80},{80,96},{96,112},{1,17},{17... | collective-permute-start | bytes 4616 | tf_op jit(solution)/shard_map/ppermute | solution.py:17
  4.5 7.0 %collective-permute-start.1 = (f32[256,1]{1,0:T(8,128)S(1)}, f32[256,1]{1,0:T(8,128)S(1)}, u32[]{:S(2)}, u32[]{:S(2)}) collective-permute-start(f32[256,1]{1,0:T(8,128)S(1)} %slice.110), channel_id=1, source_target_pairs={{0,1},{1,2},{2,3},{3,4},{4,5},{5,6},{6,7},{7,8},{8,9},{9,10},{10,1... | collective-permute-start | bytes 3080 | tf_op jit(solution)/shard_map/ppermute | solution.py:17
  34.5 62.8 %copy-start.7 = (f32[256,384]{1,0:T(8,128)S(1)}, f32[256,384]{1,0:T(8,128)}, u32[]{:S(2)}) copy-start(f32[256,384]{1,0:T(8,128)} %param.9) | copy-start | bytes 1179652
  77.0 20.2 %collective-permute-start.3 = (f32[16,1,384]{2,0,1:T(8,128)S(1)}, f32[16,1,384]{2,0,1:T(8,128)S(1)}, u32[]{:S(2)}, u32[]{:S(2)}) collective-permute-start(f32[16,1,384]{2,0,1:T(8,128)S(1)} %get-tuple-element.32), channel_id=1, source_target_pairs={{0,16},{16,32},{32,48},{48,64},{64,80},{80,96},{96,112},{1,17},{17... | collective-permute-start | bytes 73736 | tf_op jit(solution)/shard_map/ppermute | solution.py:28
  78.3 18.9 %collective-permute-start.2 = (f32[16,1,384]{2,0,1:T(8,128)S(1)}, f32[16,1,384]{2,0,1:T(8,128)S(1)}, u32[]{:S(2)}, u32[]{:S(2)}) collective-permute-start(f32[16,1,384]{2,0,1:T(8,128)S(1)} %get-tuple-element.33), channel_id=1, source_target_pairs={{16,0},{32,16},{48,32},{64,48},{80,64},{96,80},{112,96},{17,1},{33... | collective-permute-start | bytes 73736 | tf_op jit(solution)/shard_map/ppermute | solution.py:29
  83.2 11.7 %collective-permute-start.5 = (f32[16,256,1]{1,0,2:T(8,128)S(1)}, f32[16,256,1]{1,0,2:T(8,128)S(1)}, u32[]{:S(2)}, u32[]{:S(2)}) collective-permute-start(f32[16,256,1]{1,0,2:T(8,128)S(1)} %copy.224), channel_id=1, source_target_pairs={{0,1},{1,2},{2,3},{3,4},{4,5},{5,6},{6,7},{7,8},{8,9},{9,10},{10,1... | collective-permute-start | bytes 49160 | tf_op jit(solution)/shard_map/ppermute | solution.py:28
  86.8 5.6 collective-permute-start.4
  94.9 31.0 %slice-start = ((s8[6291456]{0:T(1024)(128)(4,1)}), s8[2097152]{0:T(1024)(128)(4,1)S(1)}, s32[]{:S(2)}) async-start(s8[6291456]{0:T(1024)(128)(4,1)} %bitcast.175), calls=%async_computation | async-start | bytes 4194304
  97.3 28.7 %slice-start.1 = ((s8[6291456]{0:T(1024)(128)(4,1)}), s8[4194304]{0:T(1024)(128)(4,1)S(1)}, s32[]{:S(2)}) async-start(s8[6291456]{0:T(1024)(128)(4,1)} %bitcast.175), calls=%async_computation.1 | async-start | bytes 8388608
  117.8 18.8 %copy-start.1 = (f32[16,256,384]{2,0,1:T(8,128)}, f32[16,256,384]{2,0,1:T(8,128)S(1)}, u32[]{:S(2)}) copy-start(f32[16,256,384]{2,0,1:T(8,128)S(1)} %fusion.14) | copy-start | bytes 18874372
  306.0 19.2 %collective-permute-start.7 = (f32[16,1,384]{2,0,1:T(8,128)S(1)}, f32[16,1,384]{2,0,1:T(8,128)S(1)}, u32[]{:S(2)}, u32[]{:S(2)}) collective-permute-start(f32[16,1,384]{2,0,1:T(8,128)S(1)} %get-tuple-element.28), channel_id=1, source_target_pairs={{0,16},{16,32},{32,48},{48,64},{64,80},{80,96},{96,112},{1,17},{17... | collective-permute-start | bytes 73736 | tf_op jit(solution)/shard_map/ppermute | solution.py:28
  307.3 17.9 %collective-permute-start.6 = (f32[16,1,384]{2,0,1:T(8,128)S(1)}, f32[16,1,384]{2,0,1:T(8,128)S(1)}, u32[]{:S(2)}, u32[]{:S(2)}) collective-permute-start(f32[16,1,384]{2,0,1:T(8,128)S(1)} %get-tuple-element.29), channel_id=1, source_target_pairs={{16,0},{32,16},{48,32},{64,48},{80,64},{96,80},{112,96},{17,1},{33... | collective-permute-start | bytes 73736 | tf_op jit(solution)/shard_map/ppermute | solution.py:29
  312.2 10.6 %collective-permute-start.9 = (f32[16,256,1]{1,0,2:T(8,128)S(1)}, f32[16,256,1]{1,0,2:T(8,128)S(1)}, u32[]{:S(2)}, u32[]{:S(2)}) collective-permute-start(f32[16,256,1]{1,0,2:T(8,128)S(1)} %copy.245), channel_id=1, source_target_pairs={{0,1},{1,2},{2,3},{3,4},{4,5},{5,6},{6,7},{7,8},{8,9},{9,10},{10,1... | collective-permute-start | bytes 49160 | tf_op jit(solution)/shard_map/ppermute | solution.py:28
  314.1 6.2 collective-permute-start.8
  322.8 29.1 %slice-start.6 = ((s8[6291456]{0:T(1024)(128)(4,1)}), s8[2097152]{0:T(1024)(128)(4,1)S(1)}, s32[]{:S(2)}) async-start(s8[6291456]{0:T(1024)(128)(4,1)} %bitcast.181), calls=%async_computation.6 | async-start | bytes 4194304
  325.2 26.7 %slice-start.7 = ((s8[6291456]{0:T(1024)(128)(4,1)}), s8[4194304]{0:T(1024)(128)(4,1)S(1)}, s32[]{:S(2)}) async-start(s8[6291456]{0:T(1024)(128)(4,1)} %bitcast.181), calls=%async_computation.7 | async-start | bytes 8388608
  343.7 16.2 %copy-start.2 = (f32[16,256,384]{2,0,1:T(8,128)}, f32[16,256,384]{2,0,1:T(8,128)S(1)}, u32[]{:S(2)}) copy-start(f32[16,256,384]{2,0,1:T(8,128)S(1)} %fusion.34) | copy-start | bytes 18874372
  343.7 16.2 %slice-start.4 = ((s8[6291456]{0:T(1024)(128)(4,1)}), s8[4194304]{0:T(1024)(128)(4,1)S(1)}, s32[]{:S(2)}) async-start(s8[6291456]{0:T(1024)(128)(4,1)} %bitcast.179), calls=%async_computation.4 | async-start | bytes 8388608
  351.9 8.1 %slice-start.5 = ((s8[6291456]{0:T(1024)(128)(4,1)}), s8[2097152]{0:T(1024)(128)(4,1)S(1)}, s32[]{:S(2)}) async-start(s8[6291456]{0:T(1024)(128)(4,1)} %bitcast.179), calls=%async_computation.5 | async-start | bytes 4194304
  517.7 26.3 %collective-permute-start.11 = (f32[16,1,384]{2,0,1:T(8,128)S(1)}, f32[16,1,384]{2,0,1:T(8,128)S(1)}, u32[]{:S(2)}, u32[]{:S(2)}) collective-permute-start(f32[16,1,384]{2,0,1:T(8,128)S(1)} %get-tuple-element.24), channel_id=1, source_target_pairs={{0,16},{16,32},{32,48},{48,64},{64,80},{80,96},{96,112},{1,17},{17... | collective-permute-start | bytes 73736 | tf_op jit(solution)/shard_map/ppermute | solution.py:28
  519.0 25.0 %collective-permute-start.10 = (f32[16,1,384]{2,0,1:T(8,128)S(1)}, f32[16,1,384]{2,0,1:T(8,128)S(1)}, u32[]{:S(2)}, u32[]{:S(2)}) collective-permute-start(f32[16,1,384]{2,0,1:T(8,128)S(1)} %get-tuple-element.25), channel_id=1, source_target_pairs={{16,0},{32,16},{48,32},{64,48},{80,64},{96,80},{112,96},{17,1},{33... | collective-permute-start | bytes 73736 | tf_op jit(solution)/shard_map/ppermute | solution.py:29
  523.9 20.2 %copy-start.8 = (f32[256,384]{1,0:T(8,128)S(1)}, f32[256,384]{1,0:T(8,128)}, u32[]{:S(2)}) copy-start(f32[256,384]{1,0:T(8,128)} %param.8) | copy-start | bytes 1179652
  523.9 20.2 %copy-start.9 = (f32[256,384]{1,0:T(8,128)S(1)}, f32[256,384]{1,0:T(8,128)}, u32[]{:S(2)}) copy-start(f32[256,384]{1,0:T(8,128)} %convert_element_type.10) | copy-start | bytes 1179652
  523.9 20.2 %copy-start.10 = (f32[256,384]{1,0:T(8,128)S(1)}, f32[256,384]{1,0:T(8,128)}, u32[]{:S(2)}) copy-start(f32[256,384]{1,0:T(8,128)} %get-tuple-element.18) | copy-start | bytes 1179652
  523.9 20.2 %copy-start.11 = (f32[256,384]{1,0:T(8,128)S(1)}, f32[256,384]{1,0:T(8,128)}, u32[]{:S(2)}) copy-start(f32[256,384]{1,0:T(8,128)} %get-tuple-element.20) | copy-start | bytes 1179652
  523.9 20.2 %copy-start.12 = (f32[256,384]{1,0:T(8,128)S(1)}, f32[256,384]{1,0:T(8,128)}, u32[]{:S(2)}) copy-start(f32[256,384]{1,0:T(8,128)} %get-tuple-element.21) | copy-start | bytes 1179652
  523.9 17.8 %collective-permute-start.13 = (f32[16,256,1]{1,0,2:T(8,128)S(1)}, f32[16,256,1]{1,0,2:T(8,128)S(1)}, u32[]{:S(2)}, u32[]{:S(2)}) collective-permute-start(f32[16,256,1]{1,0,2:T(8,128)S(1)} %copy.256), channel_id=1, source_target_pairs={{0,1},{1,2},{2,3},{3,4},{4,5},{5,6},{6,7},{7,8},{8,9},{9,10},{10,1... | collective-permute-start | bytes 49160 | tf_op jit(solution)/shard_map/ppermute | solution.py:28
  525.9 13.4 %collective-permute-start.12 = (f32[16,256,1]{1,0,2:T(8,128)S(1)}, f32[16,256,1]{1,0,2:T(8,128)S(1)}, u32[]{:S(2)}, u32[]{:S(2)}) collective-permute-start(f32[16,256,1]{1,0,2:T(8,128)S(1)} %copy.254), channel_id=1, source_target_pairs={{1,0},{2,1},{3,2},{4,3},{5,4},{6,5},{7,6},{8,7},{9,8},{10,9},{11,1... | collective-permute-start | bytes 49160 | tf_op jit(solution)/shard_map/ppermute | solution.py:29
  562.2 12.3 %copy-start.3 = (f32[16,256,384]{2,0,1:T(8,128)}, f32[16,256,384]{2,0,1:T(8,128)S(1)}, u32[]{:S(2)}) copy-start(f32[16,256,384]{2,0,1:T(8,128)S(1)} %fusion.22) | copy-start | bytes 18874372
  562.2 74.5 %slice-start.2 = ((s8[6291456]{0:T(1024)(128)(4,1)}), s8[2097152]{0:T(1024)(128)(4,1)S(1)}, s32[]{:S(2)}) async-start(s8[6291456]{0:T(1024)(128)(4,1)} %bitcast.177), calls=%async_computation.2 | async-start | bytes 4194304
  619.7 17.0 %slice-start.3 = ((s8[6291456]{0:T(1024)(128)(4,1)}), s8[4194304]{0:T(1024)(128)(4,1)S(1)}, s32[]{:S(2)}) async-start(s8[6291456]{0:T(1024)(128)(4,1)} %bitcast.177), calls=%async_computation.3 | async-start | bytes 8388608
  (3 other events, 8.0 us)
